TPU v7x, 32 devices: a whole 2x2x4 slice. The times are simulated.
32 devices in a mesh: row: 4 (over y, core), col: 8 (over z, x).
Axes of the slice: x: 2, y: 2, z: 4, core: 2. Of those that a mesh axis runs over, the one named last changes fastest.
Arguments:
- nodes: bfloat16 [32768, 512], P(('row', 'col')), may hold values from -8 to 8
- ln1_gain: float32 [512], replicated, may hold values from 0.25 to 1.75
- w_qkv: bfloat16 [512, 1536], replicated, may hold values from -1 to 1
- w_out: bfloat16 [512, 512], replicated, may hold values from -0.25 to 0.25
- ln2_gain: float32 [512], replicated, may hold values from 0.25 to 1.75
- w_up: bfloat16 [512, 2048], replicated, may hold values from -0.25 to 0.25
- w_down: bfloat16 [2048, 512], replicated, may hold values from -0.125 to 0.125
- adjacency: int32 [32768, 128], P(('row', 'col')), may hold values 0 or 1
- remote_ids: int32 [32, 10], replicated, may hold values from 0 to 255, as said below
- remote_live: int32 [32, 10], replicated, may hold values from 0 to 1, as said below
Outputs:
- updated: bfloat16 [32768, 512], P(('row', 'col'))
Inputs may be any that keep to these rules, and one draw needn't show every extreme that they name: `remote_ids`: every entry of device d's list names a block of another device in d's row or d's column of the mesh; the entries of one list are distinct; at most 1 live entries of one list name blocks of one device, and some list has exactly 1 from one device. `remote_live`: some device has all 10 entries live; every device has 8 or more.
All inputs are finite; a program needn't handle non-finite values. No bound on the sum of `adjacency` on one device may be relied on, other than what follows from the above.
Results may differ from a plain program's by a relative error of at most 0.005.
Values may be sent and summed in bfloat16 or wider, within the bound.
A program may use at most 128 MiB of HBM per device.

v0:
```python
import math

import jax
import jax.numpy as jnp
from jax import lax
from jax.sharding import PartitionSpec as P

HEADS = 8
BLK = 128
CAP = 1


EPS = 1e-05
NEG_FILL = -1e30


def normalize(values, gain):
    values = values.astype(jnp.float32)
    row_mean = jnp.mean(values, axis=-1, keepdims=True)
    centered = values - row_mean
    row_var = jnp.mean(centered * centered, axis=-1, keepdims=True)
    return (centered * lax.rsqrt(row_var + EPS) * gain).astype(jnp.bfloat16)


def attend(queries, local_kv, remote_kv, adj_rows, key_alive):
    row_count = queries.shape[0]
    model_width = queries.shape[1]
    head_dim = model_width // HEADS
    block_count = row_count // BLK
    score_scale = 1.0 / math.sqrt(head_dim)
    query_h = queries.reshape(block_count, BLK, HEADS, head_dim)
    local_keys = local_kv[:, :model_width].reshape(block_count, BLK, HEADS, head_dim)
    local_vals = local_kv[:, model_width:].reshape(block_count, BLK, HEADS, head_dim)
    remote_keys = remote_kv[:, :model_width].reshape(-1, HEADS, head_dim)
    remote_vals = remote_kv[:, model_width:].reshape(-1, HEADS, head_dim)
    local_scores = (
        jnp.einsum("bihd,bjhd->bhij", query_h, local_keys, preferred_element_type=jnp.float32)
        * score_scale
    )
    eye_mask = jnp.arange(BLK)[:, None] == jnp.arange(BLK)[None, :]
    allowed = (adj_rows.reshape(block_count, BLK, BLK) > 0) | eye_mask[None]
    local_scores = jnp.where(allowed[:, None], local_scores, NEG_FILL)
    remote_scores = (
        jnp.einsum("bihd,jhd->bhij", query_h, remote_keys, preferred_element_type=jnp.float32)
        * score_scale
    )
    remote_scores = jnp.where(key_alive[None, None, None, :] > 0, remote_scores, NEG_FILL)
    row_max = jnp.maximum(jnp.max(local_scores, axis=-1), jnp.max(remote_scores, axis=-1))
    local_exp = jnp.exp(local_scores - row_max[..., None])
    remote_exp = jnp.exp(remote_scores - row_max[..., None])
    row_total = jnp.sum(local_exp, axis=-1) + jnp.sum(remote_exp, axis=-1)
    local_probs = (local_exp / row_total[..., None]).astype(jnp.bfloat16)
    remote_probs = (remote_exp / row_total[..., None]).astype(jnp.bfloat16)
    summed = jnp.einsum(
        "bhij,bjhd->bihd", local_probs, local_vals, preferred_element_type=jnp.float32
    )
    summed = summed + jnp.einsum(
        "bhij,jhd->bihd", remote_probs, remote_vals, preferred_element_type=jnp.float32
    )
    return summed.reshape(row_count, model_width).astype(jnp.bfloat16)


def choose_blocks(owner_rows, rank_rows, alive_rows, local_rows, self_index):
    cap_iota = jnp.arange(CAP, dtype=jnp.int32)
    matched = (
        alive_rows[:, None, :]
        & (owner_rows[:, None, :] == self_index)
        & (rank_rows[:, None, :] == cap_iota[None, :, None])
    )
    return jnp.sum(matched.astype(jnp.int32) * local_rows[:, None, :], axis=2)


def outgoing(source, chosen_local, peer_count):
    picked = jnp.take(source, chosen_local.reshape(-1), axis=0, mode="clip")
    return picked.reshape(peer_count, CAP, BLK, source.shape[2])


def shards(
    nodes, ln1_gain, w_qkv, w_out, ln2_gain, w_up, w_down, adjacency, remote_ids, remote_live
):
    model_width = nodes.shape[1]
    node_count = nodes.shape[0]
    local_blocks = node_count // BLK
    slot_count = remote_ids.shape[1]
    row_size = lax.axis_size("row")
    col_size = lax.axis_size("col")
    my_row = lax.axis_index("row")
    my_col = lax.axis_index("col")
    self_index = my_row * col_size + my_col
    normed = normalize(nodes, ln1_gain)
    projected = jnp.dot(normed, w_qkv, preferred_element_type=jnp.float32).astype(jnp.bfloat16)
    queries = projected[:, :model_width]
    keyval = projected[:, model_width:]
    owner_dev = remote_ids // local_blocks
    local_slot = remote_ids % local_blocks
    alive_all = remote_live > 0
    same_owner = owner_dev[:, :, None] == owner_dev[:, None, :]
    slot_iota = jnp.arange(slot_count, dtype=jnp.int32)
    earlier = slot_iota[:, None] < slot_iota[None, :]
    slot_rank = jnp.sum(
        (same_owner & earlier[None] & alive_all[:, :, None]).astype(jnp.int32), axis=1
    )
    row_start = my_row * col_size
    col_pick = choose_blocks(
        lax.dynamic_slice_in_dim(owner_dev, row_start, col_size, 0),
        lax.dynamic_slice_in_dim(slot_rank, row_start, col_size, 0),
        lax.dynamic_slice_in_dim(alive_all, row_start, col_size, 0),
        lax.dynamic_slice_in_dim(local_slot, row_start, col_size, 0),
        self_index,
    )

    def column_of(table):
        return lax.dynamic_index_in_dim(
            table.reshape(row_size, col_size, slot_count), my_col, 1, keepdims=False
        )

    row_pick = choose_blocks(
        column_of(owner_dev),
        column_of(slot_rank),
        column_of(alive_all),
        column_of(local_slot),
        self_index,
    )
    source = normed.reshape(local_blocks, BLK, model_width)
    col_recv = lax.all_to_all(
        outgoing(source, col_pick, col_size), "col", split_axis=0, concat_axis=0, tiled=True
    )
    row_recv = lax.all_to_all(
        outgoing(source, row_pick, row_size), "row", split_axis=0, concat_axis=0, tiled=True
    )
    own_owner = lax.dynamic_index_in_dim(owner_dev, self_index, 0, keepdims=False)
    own_rank = jnp.minimum(
        lax.dynamic_index_in_dim(slot_rank, self_index, 0, keepdims=False), CAP - 1
    )
    own_alive = lax.dynamic_index_in_dim(remote_live, self_index, 0, keepdims=False)
    owner_row = own_owner // col_size
    owner_col = own_owner % col_size
    feature_width = col_recv.shape[3]
    from_col = jnp.take(
        col_recv.reshape(col_size * CAP, BLK, feature_width),
        owner_col * CAP + own_rank,
        axis=0,
        mode="clip",
    )
    from_row = jnp.take(
        row_recv.reshape(row_size * CAP, BLK, feature_width),
        owner_row * CAP + own_rank,
        axis=0,
        mode="clip",
    )
    gathered = jnp.where((owner_row == my_row)[:, None, None], from_col, from_row).reshape(
        slot_count * BLK, feature_width
    )
    remote_kv = jnp.dot(
        gathered, w_qkv[:, model_width:], preferred_element_type=jnp.float32
    ).astype(jnp.bfloat16)
    key_alive = jnp.repeat(own_alive, BLK)
    group_rows = 2 * BLK
    group_count = node_count // group_rows

    def one_group(pieces):
        query_part, kv_part, adj_part = pieces
        return attend(query_part, kv_part, remote_kv, adj_part, key_alive)

    mixed = lax.map(
        one_group,
        (
            queries.reshape(group_count, group_rows, model_width),
            keyval.reshape(group_count, group_rows, 2 * model_width),
            adjacency.reshape(group_count, group_rows, BLK),
        ),
    )
    mixed = mixed.reshape(node_count, model_width)
    residual = nodes.astype(jnp.float32) + jnp.dot(mixed, w_out, preferred_element_type=jnp.float32)
    normed_two = normalize(residual, ln2_gain)
    upward = jnp.dot(normed_two, w_up, preferred_element_type=jnp.float32)
    activated = jax.nn.gelu(upward, approximate=True).astype(jnp.bfloat16)
    return (residual + jnp.dot(activated, w_down, preferred_element_type=jnp.float32)).astype(
        jnp.bfloat16
    )


def solution(mesh):
    return jax.shard_map(
        shards,
        mesh=mesh,
        in_specs=(
            P(("row", "col"), None),
            P(),
            P(),
            P(),
            P(),
            P(),
            P(),
            P(("row", "col"), None),
            P(),
            P(),
        ),
        out_specs=P(("row", "col"), None),
        check_vma=False,
    )
```

profile of v0, /device:TPU:0, one launch (start us, length us, event | category | flops | bytes accessed | tf_op | source)
XLA Modules:
  0.0 227.4 jit_solution(1038354618828412443)
XLA Ops:
  3.5 2.3 %copy.143 = bf16[1024,512]{1,0:T(8,128)(2,1)} copy(bf16[1024,512]{0,1:T(8,128)(2,1)} %fusion.34) | data formatting | bytes 2097152 | tf_op jit(solution)/shard_map/reshape | solution.py:124
  6.5 2.6 %gather_fusion.2 = bf16[4,128,512]{2,1,0:T(8,128)(2,1)} fusion(bf16[8,128,512]{2,1,0:T(8,128)(2,1)} %bitcast.131, s32[1024]{0:T(1024)S(1)} %pad_clamp_fusion.1), kind=kCustom, calls=%fused_computation.2 | custom fusion | bytes 1048592 | tf_op jit(solution)/shard_map/jit(_take)/gather | solution.py:74
  9.1 4.3 %all-to-all-start.1 = ((bf16[4,1,128,512]{3,2,1,0:T(8,128)(2,1)}), bf16[4,1,128,512]{3,2,1,0:T(8,128)(2,1)}, u32[]{:S(2)}, u32[]{:S(2)}) async-start(bf16[4,1,128,512]{3,2,1,0:T(8,128)(2,1)} %bitcast.137), calls=%async_computation.1 | async-start | bytes 1048576 | tf_op jit(solution)/shard_map/all_to_all | solution.py:128
  15.1 7.7 %all-to-all-done.1 = bf16[4,1,128,512]{3,2,1,0:T(8,128)(2,1)} async-done(((bf16[4,1,128,512]{3,2,1,0:T(8,128)(2,1)}), bf16[4,1,128,512]{3,2,1,0:T(8,128)(2,1)}, u32[]{:S(2)}, u32[]{:S(2)}) %all-to-all-start.1) | async-done | bytes 524320 | tf_op jit(solution)/shard_map/all_to_all | solution.py:128
  22.9 6.6 %all-to-all-start = ((bf16[8,1,128,512]{3,2,1,0:T(8,128)(2,1)}), bf16[8,1,128,512]{3,2,1,0:T(8,128)(2,1)S(1)}, u32[]{:S(2)}, u32[]{:S(2)}) async-start(bf16[8,1,128,512]{3,2,1,0:T(8,128)(2,1)} %bitcast.135), calls=%async_computation | async-start | bytes 2097152 | tf_op jit(solution)/shard_map/all_to_all | solution.py:125
  29.4 3.6 %convolution_convert_fusion.1 = bf16[1024,1536]{1,0:T(8,128)(2,1)S(1)} fusion(bf16[1024,512]{0,1:T(8,128)(2,1)} %fusion.34, bf16[512,1536]{1,0:T(8,128)(2,1)} %param.14), kind=kOutput, calls=%fused_computation.50 | convolution fusion | flops 1612185600 | bytes 5767168 | tf_op jit(solution)/shard_map/dot_general | solution.py:91
  36.1 2.8 %gather_fusion.3 = bf16[10,128,512]{2,1,0:T(8,128)(2,1)} fusion(bf16[4,128,512]{2,1,0:T(8,128)(2,1)} %bitcast.11, s32[1024]{0:T(1024)S(1)} %pad_clamp_fusion), kind=kCustom, calls=%fused_computation.3 | custom fusion | bytes 2621480 | tf_op jit(solution)/shard_map/jit(_take)/gather | solution.py:145
  39.0 16.1 %all-to-all-done = bf16[8,1,128,512]{3,2,1,0:T(8,128)(2,1)S(1)} async-done(((bf16[8,1,128,512]{3,2,1,0:T(8,128)(2,1)}), bf16[8,1,128,512]{3,2,1,0:T(8,128)(2,1)S(1)}, u32[]{:S(2)}, u32[]{:S(2)}) %all-to-all-start) | async-done | bytes 1048608 | tf_op jit(solution)/shard_map/all_to_all | solution.py:125
  59.0 3.0 %convolution_convert_fusion = bf16[1280,1024]{1,0:T(8,128)(2,1)} fusion(bf16[1280,512]{1,0:T(8,128)(2,1)S(1)} %bitcast_select_fusion, bf16[512,1536]{1,0:T(8,128)(2,1)S(1)} %copy-done.11), kind=kOutput, calls=%fused_computation.49 | convolution fusion | flops 1343488000 | bytes 4980736 | tf_op jit(solution)/shard_map/dot_general | solution.py:154
  62.0 4.4 %copy.136 = bf16[1280,1024]{0,1:T(8,128)(2,1)} copy(bf16[1280,1024]{1,0:T(8,128)(2,1)} %convolution_convert_fusion) | data formatting | bytes 5242880
  66.5 147.2 %while.11 = (s32[]{:T(128)}, bf16[4,256,512]{2,1,0:T(8,128)(2,1)}, bf16[4,256,1024]{2,1,0:T(8,128)(2,1)}, s32[4,256,128]{2,1,0:T(8,128)}, bf16[4,256,512]{2,1,0:...) while((s32[]{:T(128)}, bf16[4,256,512]{2,1,0:T(8,128)(2,1)}, ...), condition=%wide.region_10.11_spmd.clone, body=%wide.region_5.10_spmd.clone.sunk | while | flops 772091904 | bytes 101979416 | solution.py:165
  66.5 3.0 %fusion.88 = (bf16[1280,512]{0,1:T(8,128)(2,1)S(1)}, bf16[1280,512]{0,1:T(8,128)(2,1)}) fusion(bf16[1280,1024]{0,1:T(8,128)(2,1)} %get-tuple-element.212), kind=kLoop, calls=%fused_computation.120.clone.1 | loop fusion | bytes 5242880 | tf_op jit(solution)/shard_map/while/body/eval_jaxpr/slice | solution.py:34
  74.7 6.5 %bitcast_reduce_fusion.2 = (f32[2,8,128]{2,0,1:T(2,128)S(1)}, f32[8,2,128,1280]{3,2,1,0:T(8,128)}) fusion(pred[1280]{0:T(1024)(128)(4,1)S(1)} %broadcast_bitcast_fusion.3, bf16[1280,8,64,1]{0,2,3,1:T(8,128)(2,1)S(1)} %bitcast.127, bf16[2,128,8,64]{1,0,3,2:T(2,128)(2,1)} %reshape.378), kind=kOutput, calls=%fused_computation.6.clone.1 | convolution fusion | flops 343406592 | bytes 12068096 | tf_op jit(solution)/shard_map/while/body/eval_jaxpr/bihd,jhd->bhij/dot_general | solution.py:44
  86.8 6.4 %fusion.92 = f32[2,8,128]{2,0,1:T(2,128)S(1)} fusion(f32[8,2,128,1280]{3,2,1,0:T(8,128)} %get-tuple-element.185, f32[2,8,128]{2,0,1:T(2,128)S(1)} %copy.193, pred[1280]{0:T(1024)(128)(4,1)S(1)} %broadcast_bitcast_fusion.3), kind=kLoop, calls=%fused_computation.10.clone.1 | loop fusion | flops 10483712 | bytes 10503424 | tf_op jit(solution)/shard_map/while/body/eval_jaxpr/reduce_sum | solution.py:51
  93.8 4.2 %fusion.93 = f32[2,128,8,64]{1,3,2,0:T(8,128)} fusion(bf16[1280,8,64,1]{0,2,1,3:T(8,128)(2,1)S(1)} %bitcast.129, f32[8,2,128,1280]{3,2,1,0:T(8,128)S(1)} %copy-done.1, f32[2,8,128]{2,0,1:T(2,128)S(1)} %copy.194, f32[2,8,128]{2,0,1:T(2,128)S(1)} %copy.193, pred[1280]{0:T(1024)(128)(4,1)S(1)} %broadcast_bitcast_fusion.3), kind=kOutput, calls=%fused_computation.15.clone.1 | convolution fusion | flops 348651520 | bytes 12338432 | tf_op jit(solution)/shard_map/while/body/eval_jaxpr/bhij,jhd->bihd/dot_general | solution.py:57
  98.8 2.2 fusion.94
  103.3 3.0 %fusion.88 = (bf16[1280,512]{0,1:T(8,128)(2,1)S(1)}, bf16[1280,512]{0,1:T(8,128)(2,1)}) fusion(bf16[1280,1024]{0,1:T(8,128)(2,1)} %get-tuple-element.212), kind=kLoop, calls=%fused_computation.120.clone.1 | loop fusion | bytes 5242880 | tf_op jit(solution)/shard_map/while/body/eval_jaxpr/slice | solution.py:34
  111.5 6.5 %bitcast_reduce_fusion.2 = (f32[2,8,128]{2,0,1:T(2,128)S(1)}, f32[8,2,128,1280]{3,2,1,0:T(8,128)}) fusion(pred[1280]{0:T(1024)(128)(4,1)S(1)} %broadcast_bitcast_fusion.3, bf16[1280,8,64,1]{0,2,3,1:T(8,128)(2,1)S(1)} %bitcast.127, bf16[2,128,8,64]{1,0,3,2:T(2,128)(2,1)} %reshape.378), kind=kOutput, calls=%fused_computation.6.clone.1 | convolution fusion | flops 343406592 | bytes 12068096 | tf_op jit(solution)/shard_map/while/body/eval_jaxpr/bihd,jhd->bhij/dot_general | solution.py:44
  123.6 6.4 %fusion.92 = f32[2,8,128]{2,0,1:T(2,128)S(1)} fusion(f32[8,2,128,1280]{3,2,1,0:T(8,128)} %get-tuple-element.185, f32[2,8,128]{2,0,1:T(2,128)S(1)} %copy.193, pred[1280]{0:T(1024)(128)(4,1)S(1)} %broadcast_bitcast_fusion.3), kind=kLoop, calls=%fused_computation.10.clone.1 | loop fusion | flops 10483712 | bytes 10503424 | tf_op jit(solution)/shard_map/while/body/eval_jaxpr/reduce_sum | solution.py:51
  130.6 4.2 %fusion.93 = f32[2,128,8,64]{1,3,2,0:T(8,128)} fusion(bf16[1280,8,64,1]{0,2,1,3:T(8,128)(2,1)S(1)} %bitcast.129, f32[8,2,128,1280]{3,2,1,0:T(8,128)S(1)} %copy-done.1, f32[2,8,128]{2,0,1:T(2,128)S(1)} %copy.194, f32[2,8,128]{2,0,1:T(2,128)S(1)} %copy.193, pred[1280]{0:T(1024)(128)(4,1)S(1)} %broadcast_bitcast_fusion.3), kind=kOutput, calls=%fused_computation.15.clone.1 | convolution fusion | flops 348651520 | bytes 12338432 | tf_op jit(solution)/shard_map/while/body/eval_jaxpr/bhij,jhd->bihd/dot_general | solution.py:57
  135.6 2.2 fusion.94
  140.0 3.0 %fusion.88 = (bf16[1280,512]{0,1:T(8,128)(2,1)S(1)}, bf16[1280,512]{0,1:T(8,128)(2,1)}) fusion(bf16[1280,1024]{0,1:T(8,128)(2,1)} %get-tuple-element.212), kind=kLoop, calls=%fused_computation.120.clone.1 | loop fusion | bytes 5242880 | tf_op jit(solution)/shard_map/while/body/eval_jaxpr/slice | solution.py:34
  148.3 6.5 %bitcast_reduce_fusion.2 = (f32[2,8,128]{2,0,1:T(2,128)S(1)}, f32[8,2,128,1280]{3,2,1,0:T(8,128)}) fusion(pred[1280]{0:T(1024)(128)(4,1)S(1)} %broadcast_bitcast_fusion.3, bf16[1280,8,64,1]{0,2,3,1:T(8,128)(2,1)S(1)} %bitcast.127, bf16[2,128,8,64]{1,0,3,2:T(2,128)(2,1)} %reshape.378), kind=kOutput, calls=%fused_computation.6.clone.1 | convolution fusion | flops 343406592 | bytes 12068096 | tf_op jit(solution)/shard_map/while/body/eval_jaxpr/bihd,jhd->bhij/dot_general | solution.py:44
  160.4 6.4 %fusion.92 = f32[2,8,128]{2,0,1:T(2,128)S(1)} fusion(f32[8,2,128,1280]{3,2,1,0:T(8,128)} %get-tuple-element.185, f32[2,8,128]{2,0,1:T(2,128)S(1)} %copy.193, pred[1280]{0:T(1024)(128)(4,1)S(1)} %broadcast_bitcast_fusion.3), kind=kLoop, calls=%fused_computation.10.clone.1 | loop fusion | flops 10483712 | bytes 10503424 | tf_op jit(solution)/shard_map/while/body/eval_jaxpr/reduce_sum | solution.py:51
  167.4 4.2 %fusion.93 = f32[2,128,8,64]{1,3,2,0:T(8,128)} fusion(bf16[1280,8,64,1]{0,2,1,3:T(8,128)(2,1)S(1)} %bitcast.129, f32[8,2,128,1280]{3,2,1,0:T(8,128)S(1)} %copy-done.1, f32[2,8,128]{2,0,1:T(2,128)S(1)} %copy.194, f32[2,8,128]{2,0,1:T(2,128)S(1)} %copy.193, pred[1280]{0:T(1024)(128)(4,1)S(1)} %broadcast_bitcast_fusion.3), kind=kOutput, calls=%fused_computation.15.clone.1 | convolution fusion | flops 348651520 | bytes 12338432 | tf_op jit(solution)/shard_map/while/body/eval_jaxpr/bhij,jhd->bihd/dot_general | solution.py:57
  172.4 2.2 fusion.94
  176.8 3.0 %fusion.88 = (bf16[1280,512]{0,1:T(8,128)(2,1)S(1)}, bf16[1280,512]{0,1:T(8,128)(2,1)}) fusion(bf16[1280,1024]{0,1:T(8,128)(2,1)} %get-tuple-element.212), kind=kLoop, calls=%fused_computation.120.clone.1 | loop fusion | bytes 5242880 | tf_op jit(solution)/shard_map/while/body/eval_jaxpr/slice | solution.py:34
  185.1 6.5 %bitcast_reduce_fusion.2 = (f32[2,8,128]{2,0,1:T(2,128)S(1)}, f32[8,2,128,1280]{3,2,1,0:T(8,128)}) fusion(pred[1280]{0:T(1024)(128)(4,1)S(1)} %broadcast_bitcast_fusion.3, bf16[1280,8,64,1]{0,2,3,1:T(8,128)(2,1)S(1)} %bitcast.127, bf16[2,128,8,64]{1,0,3,2:T(2,128)(2,1)} %reshape.378), kind=kOutput, calls=%fused_computation.6.clone.1 | convolution fusion | flops 343406592 | bytes 12068096 | tf_op jit(solution)/shard_map/while/body/eval_jaxpr/bihd,jhd->bhij/dot_general | solution.py:44
  197.2 6.4 %fusion.92 = f32[2,8,128]{2,0,1:T(2,128)S(1)} fusion(f32[8,2,128,1280]{3,2,1,0:T(8,128)} %get-tuple-element.185, f32[2,8,128]{2,0,1:T(2,128)S(1)} %copy.193, pred[1280]{0:T(1024)(128)(4,1)S(1)} %broadcast_bitcast_fusion.3), kind=kLoop, calls=%fused_computation.10.clone.1 | loop fusion | flops 10483712 | bytes 10503424 | tf_op jit(solution)/shard_map/while/body/eval_jaxpr/reduce_sum | solution.py:51
  204.2 4.2 %fusion.93 = f32[2,128,8,64]{1,3,2,0:T(8,128)} fusion(bf16[1280,8,64,1]{0,2,1,3:T(8,128)(2,1)S(1)} %bitcast.129, f32[8,2,128,1280]{3,2,1,0:T(8,128)S(1)} %copy-done.1, f32[2,8,128]{2,0,1:T(2,128)S(1)} %copy.194, f32[2,8,128]{2,0,1:T(2,128)S(1)} %copy.193, pred[1280]{0:T(1024)(128)(4,1)S(1)} %broadcast_bitcast_fusion.3), kind=kOutput, calls=%fused_computation.15.clone.1 | convolution fusion | flops 348651520 | bytes 12338432 | tf_op jit(solution)/shard_map/while/body/eval_jaxpr/bhij,jhd->bihd/dot_general | solution.py:57
  213.6 2.5 %fusion.63 = (f32[1024]{0:T(1024)S(1)}, f32[1024,512]{0,1:T(8,128)S(1)}) fusion(bf16[1024,512]{1,0:T(8,128)(2,1)} %bitcast.138, bf16[512,512]{1,0:T(8,128)(2,1)} %param.15, bf16[1024,512]{0,1:T(8,128)(2,1)} %copy-done.4), kind=kOutput, calls=%fused_computation.123 | convolution fusion | flops 538442752 | bytes 4722688 | tf_op jit(solution)/shard_map/dot_general | solution.py:174
  217.8 8.3 %add_convert_fusion = bf16[1024,512]{0,1:T(8,128)(2,1)S(1)} fusion(f32[1024,512]{0,1:T(8,128)} %copy-done.6, bf16[2048,512]{1,0:T(8,128)(2,1)S(1)} %copy-done, bf16[512,2048]{1,0:T(8,128)(2,1)} %param.17, f32[512]{0:T(512)S(1)} %copy-done.12, f32[1024]{0:T(1024)S(1)} %add_rsqrt_fusion, f32[1024]{0:T(1024)S(1)} %broadcast_multiply_fusion), kind=kOutput, calls=%fused_computation.59 | convolution fusion | flops 4316987392 | bytes 7350272 | tf_op jit(solution)/shard_map/dot_general | solution.py:178
  (178 shorter events, 75.7 us)
Async XLA Ops:
  0.0 217.8 %copy-start = (bf16[2048,512]{1,0:T(8,128)(2,1)S(1)}, bf16[2048,512]{1,0:T(8,128)(2,1)}, u32[]{:S(2)}) copy-start(bf16[2048,512]{1,0:T(8,128)(2,1)} %param.18) | copy-start | bytes 6291460
  0.0 2.2 copy-start.10
  1.7 1.9 copy-start.4
  2.2 3.6 %copy-start.9 = (s32[32,10]{0,1:T(8,128)S(1)}, s32[32,10]{0,1:T(8,128)}, u32[]{:S(2)}) copy-start(s32[32,10]{0,1:T(8,128)} %param.20) | copy-start | bytes 3844
  2.2 3.8 %copy-start.8 = (s32[32,10]{0,1:T(8,128)S(1)}, s32[32,10]{0,1:T(8,128)}, u32[]{:S(2)}) copy-start(s32[32,10]{0,1:T(8,128)} %param.21) | copy-start | bytes 3844
  5.8 7.7 %copy-start.7 = (bf16[1024,512]{1,0:T(8,128)(2,1)S(1)}, bf16[1024,512]{1,0:T(8,128)(2,1)}, u32[]{:S(2)}) copy-start(bf16[1024,512]{1,0:T(8,128)(2,1)} %copy.143) | copy-start | bytes 3145732
  9.1 13.7 %all-to-all-start.1 = ((bf16[4,1,128,512]{3,2,1,0:T(8,128)(2,1)}), bf16[4,1,128,512]{3,2,1,0:T(8,128)(2,1)}, u32[]{:S(2)}, u32[]{:S(2)}) async-start(bf16[4,1,128,512]{3,2,1,0:T(8,128)(2,1)} %bitcast.137), calls=%async_computation.1 | async-start | bytes 1048576 | tf_op jit(solution)/shard_map/all_to_all | solution.py:128
  22.9 32.2 %all-to-all-start = ((bf16[8,1,128,512]{3,2,1,0:T(8,128)(2,1)}), bf16[8,1,128,512]{3,2,1,0:T(8,128)(2,1)S(1)}, u32[]{:S(2)}, u32[]{:S(2)}) async-start(bf16[8,1,128,512]{3,2,1,0:T(8,128)(2,1)} %bitcast.135), calls=%async_computation | async-start | bytes 2097152 | tf_op jit(solution)/shard_map/all_to_all | solution.py:125
  56.8 2.2 copy-start.11
  81.2 4.0 %copy-start.2 = (bf16[2,128,8,64]{1,0,3,2:T(2,128)(2,1)S(1)}, bf16[2,128,8,64]{1,0,3,2:T(2,128)(2,1)}, u32[]{:S(2)}) copy-start(bf16[2,128,8,64]{1,0,3,2:T(2,128)(2,1)} %reshape.378) | copy-start | bytes 786436 | tf_op jit(solution)/shard_map/while
  85.2 8.0 %copy-start.3 = (bf16[1280,512]{0,1:T(8,128)(2,1)S(1)}, bf16[1280,512]{0,1:T(8,128)(2,1)}, u32[]{:S(2)}) copy-start(bf16[1280,512]{0,1:T(8,128)(2,1)} %get-tuple-element.183) | copy-start | bytes 3932164 | tf_op jit(solution)/shard_map/while
  86.8 7.0 %copy-start.1 = (f32[8,2,128,1280]{3,2,1,0:T(8,128)S(1)}, f32[8,2,128,1280]{3,2,1,0:T(8,128)}, u32[]{:S(2)}) copy-start(f32[8,2,128,1280]{3,2,1,0:T(8,128)} %get-tuple-element.185) | copy-start | bytes 31457284 | tf_op jit(solution)/shard_map/while
  93.8 4.2 %copy-start.5 = (bf16[256,512]{0,1:T(8,128)(2,1)S(1)}, bf16[256,512]{0,1:T(8,128)(2,1)}, u32[]{:S(2)}) copy-start(bf16[256,512]{0,1:T(8,128)(2,1)} %get-tuple-element.190) | copy-start | bytes 786436 | tf_op jit(solution)/shard_map/while
  118.0 4.0 %copy-start.2 = (bf16[2,128,8,64]{1,0,3,2:T(2,128)(2,1)S(1)}, bf16[2,128,8,64]{1,0,3,2:T(2,128)(2,1)}, u32[]{:S(2)}) copy-start(bf16[2,128,8,64]{1,0,3,2:T(2,128)(2,1)} %reshape.378) | copy-start | bytes 786436 | tf_op jit(solution)/shard_map/while
  122.0 8.1 %copy-start.3 = (bf16[1280,512]{0,1:T(8,128)(2,1)S(1)}, bf16[1280,512]{0,1:T(8,128)(2,1)}, u32[]{:S(2)}) copy-start(bf16[1280,512]{0,1:T(8,128)(2,1)} %get-tuple-element.183) | copy-start | bytes 3932164 | tf_op jit(solution)/shard_map/while
  123.6 7.0 %copy-start.1 = (f32[8,2,128,1280]{3,2,1,0:T(8,128)S(1)}, f32[8,2,128,1280]{3,2,1,0:T(8,128)}, u32[]{:S(2)}) copy-start(f32[8,2,128,1280]{3,2,1,0:T(8,128)} %get-tuple-element.185) | copy-start | bytes 31457284 | tf_op jit(solution)/shard_map/while
  130.6 4.2 %copy-start.5 = (bf16[256,512]{0,1:T(8,128)(2,1)S(1)}, bf16[256,512]{0,1:T(8,128)(2,1)}, u32[]{:S(2)}) copy-start(bf16[256,512]{0,1:T(8,128)(2,1)} %get-tuple-element.190) | copy-start | bytes 786436 | tf_op jit(solution)/shard_map/while
  154.8 4.0 %copy-start.2 = (bf16[2,128,8,64]{1,0,3,2:T(2,128)(2,1)S(1)}, bf16[2,128,8,64]{1,0,3,2:T(2,128)(2,1)}, u32[]{:S(2)}) copy-start(bf16[2,128,8,64]{1,0,3,2:T(2,128)(2,1)} %reshape.378) | copy-start | bytes 786436 | tf_op jit(solution)/shard_map/while
  158.8 8.1 %copy-start.3 = (bf16[1280,512]{0,1:T(8,128)(2,1)S(1)}, bf16[1280,512]{0,1:T(8,128)(2,1)}, u32[]{:S(2)}) copy-start(bf16[1280,512]{0,1:T(8,128)(2,1)} %get-tuple-element.183) | copy-start | bytes 3932164 | tf_op jit(solution)/shard_map/while
  160.4 7.0 %copy-start.1 = (f32[8,2,128,1280]{3,2,1,0:T(8,128)S(1)}, f32[8,2,128,1280]{3,2,1,0:T(8,128)}, u32[]{:S(2)}) copy-start(f32[8,2,128,1280]{3,2,1,0:T(8,128)} %get-tuple-element.185) | copy-start | bytes 31457284 | tf_op jit(solution)/shard_map/while
  167.4 4.2 %copy-start.5 = (bf16[256,512]{0,1:T(8,128)(2,1)S(1)}, bf16[256,512]{0,1:T(8,128)(2,1)}, u32[]{:S(2)}) copy-start(bf16[256,512]{0,1:T(8,128)(2,1)} %get-tuple-element.190) | copy-start | bytes 786436 | tf_op jit(solution)/shard_map/while
  191.6 4.0 %copy-start.2 = (bf16[2,128,8,64]{1,0,3,2:T(2,128)(2,1)S(1)}, bf16[2,128,8,64]{1,0,3,2:T(2,128)(2,1)}, u32[]{:S(2)}) copy-start(bf16[2,128,8,64]{1,0,3,2:T(2,128)(2,1)} %reshape.378) | copy-start | bytes 786436 | tf_op jit(solution)/shard_map/while
  195.6 8.1 %copy-start.3 = (bf16[1280,512]{0,1:T(8,128)(2,1)S(1)}, bf16[1280,512]{0,1:T(8,128)(2,1)}, u32[]{:S(2)}) copy-start(bf16[1280,512]{0,1:T(8,128)(2,1)} %get-tuple-element.183) | copy-start | bytes 3932164 | tf_op jit(solution)/shard_map/while
  197.2 7.0 %copy-start.1 = (f32[8,2,128,1280]{3,2,1,0:T(8,128)S(1)}, f32[8,2,128,1280]{3,2,1,0:T(8,128)}, u32[]{:S(2)}) copy-start(f32[8,2,128,1280]{3,2,1,0:T(8,128)} %get-tuple-element.185) | copy-start | bytes 31457284 | tf_op jit(solution)/shard_map/while
  204.2 4.2 %copy-start.5 = (bf16[256,512]{0,1:T(8,128)(2,1)S(1)}, bf16[256,512]{0,1:T(8,128)(2,1)}, u32[]{:S(2)}) copy-start(bf16[256,512]{0,1:T(8,128)(2,1)} %get-tuple-element.190) | copy-start | bytes 786436 | tf_op jit(solution)/shard_map/while
  216.1 1.4 copy-start.6
  216.1 1.7 copy-start.12
where the time goes:
time: 229 us; the launch traced here: 227 us
  local copies, waits for them, and re-layouts  82.4 us (36%)
  matrix products  74.7 us (33%)
  other arithmetic  35 us (15%)
  waiting for transfers between devices  23.8 us (10%)
  starting transfers between devices  10.8 us (5%)
    dot_general x4, matrix products, attend(): jnp.einsum('bihd,jhd->bhij', query_h, remote_keys, preferred_element_type...  26.2 us
    reduce_sum x8, other arithmetic, attend(): row_total = jnp.sum(local_exp, axis=-1) + jnp.sum(remote_exp, axis=-1)  26.2 us
    dynamic_slice x16, local copies, waits for them, and re-layouts, shards(): lax.map(one_group, (queries.reshape(group_count, group_rows, model_width)...  19.1 us
    dot_general x4, matrix products, attend(): jnp.einsum('bhij,jhd->bihd', remote_probs, remote_vals, preferred_element...  16.9 us
    all_to_all x1, waiting for transfers between devices, shards(): lax.all_to_all(outgoing(source, col_pick, col_size), 'col', split_axis=0,...  16.1 us
    slice x4, local copies, waits for them, and re-layouts, attend(): remote_keys = remote_kv[:, :model_width].reshape(-1, HEADS, head_dim)  11.9 us
    dynamic_update_slice x12, local copies, waits for them, and re-layouts, shards(): lax.map(one_group, (queries.reshape(group_count, group_rows, model_width)...  9.18 us
    dot_general x4, matrix products, attend(): jnp.einsum('bhij,bjhd->bihd', local_probs, local_vals, preferred_element_...  8.63 us
  transfers between devices with their start and end apart: 2, of which 2 were waited for; matrix products, arithmetic and copies ran while one was open for 5% of the time, Pallas kernels for 0%

commit v1 on v0

v1 whole, which is shorter than its diff:
```python
import functools
import math

import jax
import jax.numpy as jnp
from jax import lax
from jax.experimental import pallas as pl
from jax.experimental.pallas import tpu as pltpu
from jax.sharding import PartitionSpec as P

HEADS = 8
BLK = 128
HEAD_DIM = 64
AUG = 80
EPS = 1e-05
NEG_FILL = -1e30
LOG2E = 1.4426950408889634
MESH = pl.DeviceIdType.MESH
NT = (((1,), (1,)), ((), ()))


def dot(a, b):
    return jnp.dot(a, b, preferred_element_type=jnp.float32)


def dot_nt(a, b):
    return lax.dot_general(a, b, NT, preferred_element_type=jnp.float32)


def normalize(values, gain):
    values = values.astype(jnp.float32)
    row_mean = jnp.mean(values, axis=-1, keepdims=True)
    centered = values - row_mean
    row_var = jnp.mean(centered * centered, axis=-1, keepdims=True)
    return (centered * lax.rsqrt(row_var + EPS) * gain).astype(jnp.bfloat16)


def peer_offsets(row_size, col_size):
    return [("row", d) for d in range(1, row_size)] + [("col", d) for d in range(1, col_size)]


def attention_kernel(
    row_size, col_size,
    ids_ref, live_ref, nodes_ref, gain_ref, w_ref, adj_ref,
    mixed_ref,
    send_buf, recv_buf, dead_ref, wq_t, wv_t, q_t, keys, vals_t, keys_r, vals_r, bias_t, top, acc,
    send_sem, recv_sem,
):
    rows, width = nodes_ref.shape
    local_blocks = rows // BLK
    slots = ids_ref.shape[1]
    pairs = HEADS // 2
    my_row = lax.axis_index("row")
    my_col = lax.axis_index("col")
    me = my_row * col_size + my_col
    offsets = peer_offsets(row_size, col_size)
    count = len(offsets)
    group = 2 if count % 2 == 0 else 1

    def target(axis, d):
        if axis == "row":
            return lax.rem(my_row + d, row_size), my_col
        return my_row, lax.rem(my_col + d, col_size)

    def source(axis, d):
        if axis == "row":
            return lax.rem(my_row + row_size - d, row_size), my_col
        return my_row, lax.rem(my_col + col_size - d, col_size)

    barrier = pltpu.get_barrier_semaphore()
    for axis, d in offsets:
        pl.semaphore_signal(barrier, inc=1, device_id=target(axis, d), device_id_type=MESH)
    for p, (axis, d) in enumerate(offsets):
        t_row, t_col = target(axis, d)
        peer = t_row * col_size + t_col
        base = me * local_blocks
        picked = jnp.zeros((BLK, width), jnp.bfloat16)
        for b in range(local_blocks):
            hits = jnp.int32(0)
            for s in range(slots):
                hit = (live_ref[peer, s] > 0) & (ids_ref[peer, s] == base + b)
                hits = jnp.maximum(hits, hit.astype(jnp.int32))
            weight = jnp.full((1, width), hits).astype(jnp.bfloat16)
            picked = picked + nodes_ref[b * BLK : (b + 1) * BLK, :] * weight
        send_buf[p] = picked
    pl.semaphore_wait(barrier, count)

    def copy(p, device):
        return pltpu.make_async_remote_copy(
            src_ref=send_buf.at[p], dst_ref=recv_buf.at[p],
            send_sem=send_sem.at[p], recv_sem=recv_sem.at[p],
            device_id=device, device_id_type=MESH,
        )

    for p, (axis, d) in enumerate(offsets):
        copy(p, target(axis, d)).start()

    for p, (axis, d) in enumerate(offsets):
        s_row, s_col = source(axis, d)
        first = (s_row * col_size + s_col) * local_blocks
        dead = jnp.float32(NEG_FILL)
        for s in range(slots):
            block = ids_ref[me, s] - first
            hit = (live_ref[me, s] > 0) & (block >= 0) & (block < local_blocks)
            dead = jnp.where(hit, jnp.float32(0), dead)
        dead_ref[p] = dead

    gain = gain_ref[...]
    wq_t[...] = w_ref[:, :width].T
    wv_t[...] = w_ref[:, 2 * width :].T
    chunk = 2 * BLK
    score_scale = LOG2E / math.sqrt(HEAD_DIM)
    zeros = jnp.zeros((HEAD_DIM, chunk), jnp.bfloat16)
    vals_t[:, HEAD_DIM:, :] = jnp.ones((HEADS, AUG - HEAD_DIM, rows), jnp.bfloat16)
    vals_r[:, HEAD_DIM:, :] = jnp.ones((HEADS, AUG - HEAD_DIM, group * BLK), jnp.bfloat16)

    def project_local(i, carry):
        span = pl.ds(pl.multiple_of(i * chunk, chunk), chunk)
        normed = normalize(nodes_ref[span, :], gain)
        query = (dot_nt(wq_t[...], normed) * score_scale).astype(jnp.bfloat16)
        for h in range(HEADS):
            own = (h % 2) * HEAD_DIM
            q_t[h, own : own + HEAD_DIM, span] = query[h * HEAD_DIM : (h + 1) * HEAD_DIM]
            q_t[h, HEAD_DIM - own : 2 * HEAD_DIM - own, span] = zeros
        key = dot(normed, w_ref[:, width : 2 * width]).astype(jnp.bfloat16)
        for j in range(pairs):
            keys[j, span, :] = key[:, j * BLK : (j + 1) * BLK]
        value = dot_nt(wv_t[...], normed).astype(jnp.bfloat16)
        for h in range(HEADS):
            vals_t[h, :HEAD_DIM, span] = value[h * HEAD_DIM : (h + 1) * HEAD_DIM]
        return carry

    lax.fori_loop(0, rows // chunk, project_local, 0)

    eye = lax.broadcasted_iota(jnp.int32, (BLK, BLK), 0) == lax.broadcasted_iota(
        jnp.int32, (BLK, BLK), 1
    )
    for b in range(local_blocks):
        allowed = (adj_ref[b * BLK : (b + 1) * BLK, :] > 0) | eye
        bias_t[:, b * BLK : (b + 1) * BLK] = jnp.where(allowed, 0.0, NEG_FILL).T

    def attend_local(h, carry):
        for b in range(local_blocks):
            span = slice(b * BLK, (b + 1) * BLK)
            score = dot(keys[h // 2, span, :], q_t[h, :, span]) + bias_t[:, span]
            high = jnp.max(score, axis=0, keepdims=True)
            prob = jnp.exp2(score - high).astype(jnp.bfloat16)
            top[h, :, span] = high
            acc[h, :, span] = dot(vals_t[h, :, span], prob)
        return carry

    lax.fori_loop(0, HEADS, attend_local, 0)

    def attend_remote(g, carry):
        for k in range(group):
            copy(g * group + k, (my_row, my_col)).wait_recv()
        for k in range(group):
            span = slice(k * BLK, (k + 1) * BLK)
            normed = normalize(recv_buf[g * group + k], gain)
            key = dot(normed, w_ref[:, width : 2 * width]).astype(jnp.bfloat16)
            for j in range(pairs):
                keys_r[j, span, :] = key[:, j * BLK : (j + 1) * BLK]
            value = dot_nt(wv_t[...], normed).astype(jnp.bfloat16)
            for h in range(HEADS):
                vals_r[h, :HEAD_DIM, span] = value[h * HEAD_DIM : (h + 1) * HEAD_DIM]
        deads = [dead_ref[g * group + k] for k in range(group)]

        def one_head(h, inner):
            for c in range(rows // chunk):
                span = slice(c * chunk, (c + 1) * chunk)
                score = dot(keys_r[h // 2], q_t[h, :, span])
                parts = [score[k * BLK : (k + 1) * BLK] for k in range(group)]
                old = top[h, :, span]
                high = old
                for part, dead in zip(parts, deads):
                    high = jnp.maximum(high, jnp.max(part, axis=0, keepdims=True) + dead)
                prob = jnp.concatenate(
                    [
                        jnp.exp2(part - (high - dead)).astype(jnp.bfloat16)
                        for part, dead in zip(parts, deads)
                    ],
                    axis=0,
                )
                top[h, :, span] = high
                acc[h, :, span] = acc[h, :, span] * jnp.exp2(old - high) + dot(vals_r[h], prob)
            return inner

        return lax.fori_loop(0, HEADS, one_head, carry)

    lax.fori_loop(0, count // group, attend_remote, 0)

    def finish(h, carry):
        total = acc[h, HEAD_DIM : HEAD_DIM + 1, :]
        mixed_ref[h] = (acc[h, :HEAD_DIM, :] / total).astype(jnp.bfloat16)
        return carry

    lax.fori_loop(0, HEADS, finish, 0)
    for p, (axis, d) in enumerate(offsets):
        copy(p, target(axis, d)).wait_send()


def feed_kernel(mixed_ref, nodes_ref, w_out_ref, gain_ref, w_up_ref, w_down_ref, out_ref):
    mixed_t = mixed_ref[...].reshape(nodes_ref.shape[1], nodes_ref.shape[0])
    residual = nodes_ref[...].astype(jnp.float32) + dot(mixed_t.T, w_out_ref[...])
    normed = normalize(residual, gain_ref[...])
    upward = dot(normed, w_up_ref[...])
    activated = jax.nn.gelu(upward, approximate=True).astype(jnp.bfloat16)
    out_ref[...] = (residual + dot(activated, w_down_ref[...])).astype(jnp.bfloat16)


def shards(
    row_size, col_size,
    nodes, ln1_gain, w_qkv, w_out, ln2_gain, w_up, w_down, adjacency, remote_ids, remote_live
):
    rows, width = nodes.shape
    count = row_size + col_size - 2
    group = 2 if count % 2 == 0 else 1
    vmem = pl.BlockSpec(memory_space=pltpu.VMEM)
    smem = pl.BlockSpec(memory_space=pltpu.SMEM)
    bf16, f32 = jnp.bfloat16, jnp.float32
    mixed = pl.pallas_call(
        functools.partial(attention_kernel, row_size, col_size),
        out_shape=jax.ShapeDtypeStruct((HEADS, HEAD_DIM, rows), bf16),
        in_specs=[smem, smem, vmem, vmem, vmem, vmem],
        out_specs=vmem,
        scratch_shapes=[
            pltpu.VMEM((count, BLK, width), bf16),
            pltpu.VMEM((count, BLK, width), bf16),
            pltpu.SMEM((count,), f32),
            pltpu.VMEM((width, width), bf16),
            pltpu.VMEM((width, width), bf16),
            pltpu.VMEM((HEADS, 2 * HEAD_DIM, rows), bf16),
            pltpu.VMEM((HEADS // 2, rows, BLK), bf16),
            pltpu.VMEM((HEADS, AUG, rows), bf16),
            pltpu.VMEM((HEADS // 2, group * BLK, BLK), bf16),
            pltpu.VMEM((HEADS, AUG, group * BLK), bf16),
            pltpu.VMEM((BLK, rows), f32),
            pltpu.VMEM((HEADS, 1, rows), f32),
            pltpu.VMEM((HEADS, AUG, rows), f32),
            pltpu.SemaphoreType.DMA((count,)),
            pltpu.SemaphoreType.DMA((count,)),
        ],
        compiler_params=pltpu.CompilerParams(
            collective_id=0, has_side_effects=True, vmem_limit_bytes=40 << 20
        ),
        name="attention",
    )(remote_ids, remote_live, nodes, ln1_gain.reshape(1, width), w_qkv, adjacency)
    chunk = 2 * BLK
    hidden = w_up.shape[1]
    whole = lambda *dims: pl.BlockSpec(dims, lambda i: (0,) * len(dims))
    return pl.pallas_call(
        feed_kernel,
        grid=(rows // chunk,),
        out_shape=jax.ShapeDtypeStruct((rows, width), bf16),
        in_specs=[
            pl.BlockSpec((HEADS, HEAD_DIM, chunk), lambda i: (0, 0, i)),
            pl.BlockSpec((chunk, width), lambda i: (i, 0)),
            whole(width, width),
            whole(1, width),
            whole(width, hidden),
            whole(hidden, width),
        ],
        out_specs=pl.BlockSpec((chunk, width), lambda i: (i, 0)),
        compiler_params=pltpu.CompilerParams(vmem_limit_bytes=40 << 20),
        name="feed",
    )(mixed, nodes, w_out, ln2_gain.reshape(1, width), w_up, w_down)


def solution(mesh):
    split = P(("row", "col"), None)
    return jax.shard_map(
        functools.partial(shards, mesh.shape["row"], mesh.shape["col"]),
        mesh=mesh,
        in_specs=(split, P(), P(), P(), P(), P(), P(), split, P(), P()),
        out_specs=split,
        check_vma=False,
    )
```

time: 229 us -> 85.2 us (0.37)
  Pallas kernels: 0 us -> 77.3 us
  local copies, waits for them, and re-layouts: 82.4 us -> 7.5 us
  matrix products: 74.7 us -> 0 us
  other arithmetic: 35 us -> 0 us
  waiting for transfers between devices: 23.8 us -> 0 us
  starting transfers between devices: 10.8 us -> 0 us
    pallas_call x0 -> x2, Pallas kernels: none -> 77.3 us  [the longest x1 68.4 us: shards(): pl.pallas_call(functools.partial(attention_kernel, row_size, col_size), o...]
    dot_general x20 -> x0, matrix products: 74.7 us -> none  [the longest x4 26.2 us: attend(): jnp.einsum('bihd,jhd->bhij', query_h, remote_keys, preferred_element_type...]
    reduce_sum x14 -> x0, other arithmetic: 27.4 us -> none  [the longest x8 26.2 us: attend(): row_total = jnp.sum(local_exp, axis=-1) + jnp.sum(remote_exp, axis=-1)]
    all_to_all x2 -> x0, waiting for transfers between devices: 23.8 us -> none  [the longest x1 16.1 us: shards(): lax.all_to_all(outgoing(source, col_pick, col_size), 'col', split_axis=0,...]
    dynamic_slice x17 -> x0, local copies, waits for them, and re-layouts: 19.3 us -> none  [the longest x16 19.1 us: shards(): lax.map(one_group, (queries.reshape(group_count, group_rows, model_width)...]
    slice x10 -> x0, local copies, waits for them, and re-layouts: 17.5 us -> none  [the longest x4 11.9 us: attend(): remote_keys = remote_kv[:, :model_width].reshape(-1, HEADS, head_dim)]
    reshape x17 -> x0, local copies, waits for them, and re-layouts: 15.7 us -> none  [the longest x4 6.91 us: attend(): query_h = queries.reshape(block_count, BLK, HEADS, head_dim)]
    all_to_all x2 -> x0, starting transfers between devices: 10.9 us -> none  [the longest x1 6.58 us: shards(): lax.all_to_all(outgoing(source, col_pick, col_size), 'col', split_axis=0,...]
  transfers between devices with their start and end apart: 2 -> 0, of which waited for: 2 -> 0; matrix products, arithmetic and copies ran while one was open for 5% -> 0% of each run, Pallas kernels for 0% -> 0%
where the time goes in v1:
time: 85.2 us; the launch traced here: 84.9 us
  Pallas kernels  77.3 us (91%)
  local copies, waits for them, and re-layouts  7.5 us (9%)
    pallas_call x1, Pallas kernels, shards(): pl.pallas_call(functools.partial(attention_kernel, row_size, col_size), o...  68.4 us
    pallas_call x1, Pallas kernels, shards(): pl.pallas_call(feed_kernel, grid=(rows // chunk,), out_shape=jax.ShapeDty...  8.89 us
    unnamed x20, local copies, waits for them, and re-layouts  7.5 us

profile of v1, /device:TPU:0, one launch (start us, length us, event | category | flops | bytes accessed | tf_op | source)
XLA Modules:
  0.0 84.9 jit_solution(17779210514804548685)
XLA Ops:
  0.0 0.8 copy.11.ids_ref
  0.8 0.8 copy.12.live_ref
  1.6 0.0 copy-start
  1.6 1.2 %copy-done = bf16[1024,512]{1,0:T(8,128)(2,1)S(1)} copy-done((bf16[1024,512]{1,0:T(8,128)(2,1)S(1)}, bf16[1024,512]{1,0:T(8,128)(2,1)}, u32[]{:S(2)}) %copy-start) | copy-done | bytes 1048600
  2.8 0.0 copy-start.4
  2.8 1.4 %copy-done.4 = bf16[512,1536]{1,0:T(8,128)(2,1)S(1)} copy-done((bf16[512,1536]{1,0:T(8,128)(2,1)S(1)}, bf16[512,1536]{1,0:T(8,128)(2,1)}, u32[]{:S(2)}) %copy-start.4) | copy-done | bytes 1572888
  4.2 0.0 copy-start.6
  4.2 1.0 %copy-done.6 = s32[1024,128]{1,0:T(8,128)S(1)} copy-done((s32[1024,128]{1,0:T(8,128)S(1)}, s32[1024,128]{1,0:T(8,128)}, u32[]{:S(2)}) %copy-start.6) | copy-done | bytes 524312
  5.2 0.0 copy-start.7
  5.2 0.7 copy-done.7
  5.9 0.0 copy-start.1
  5.9 0.0 copy-start.2
  5.9 0.0 copy-start.5
  5.9 0.0 copy-start.8
  5.9 68.4 %attention.1.mixed_ref = bf16[8,64,1024]{2,1,0:T(8,128)(2,1)S(1)} custom-call(s32[32,10]{1,0:T(8,128)S(1)} %copy.11.ids_ref, s32[32,10]{1,0:T(8,128)S(1)} %copy.12.live_ref, bf16[1024,512]{1,0:T(8,128)(2,1)S(1)} %copy-done, f32[1,512]{1,0:T(1,128)S(1)} %bitcast.2, bf16[512,1536]{1,0:T(8,128)(2,1)S(1)} %copy-done.4, s32[1024,128]{1,0:T(8,128)S(1)} %copy-done.6), custom_call_target="tpu_custom_call" | custom-call | tf_op jit(solution)/shard_map/attention/pallas_call | solution.py:221
  74.4 0.0 copy-done.1
  74.4 0.0 copy-done.2
  74.4 0.0 copy-done.5
  74.4 0.0 copy-done.8
  74.4 0.0 copy-start.3
  74.4 1.6 %copy-done.3 = bf16[2048,512]{1,0:T(8,128)(2,1)S(1)} copy-done((bf16[2048,512]{1,0:T(8,128)(2,1)S(1)}, bf16[2048,512]{1,0:T(8,128)(2,1)}, u32[]{:S(2)}) %copy-start.3) | copy-done | bytes 2097176
  76.0 8.9 %feed.1 = bf16[1024,512]{1,0:T(8,128)(2,1)} custom-call(bf16[8,64,1024]{2,1,0:T(8,128)(2,1)S(1)} %attention.1.mixed_ref, bf16[1024,512]{1,0:T(8,128)(2,1)S(1)} %copy-done.1, bf16[512,512]{1,0:T(8,128)(2,1)S(1)} %copy-done.5, f32[1,512]{1,0:T(1,128)S(1)} %bitcast.3, bf16[512,2048]{1,0:T(8,128)(2,1)S(1)} %copy-done.2, bf16[2048,512]{1,0:T(8,128)(2,1)S(1)} %copy-done.3), custom_call_target="tpu_custom_call" | custom-call | tf_op jit(solution)/shard_map/feed/pallas_call | solution.py:251
Async XLA Ops:
  1.6 1.2 %copy-start = (bf16[1024,512]{1,0:T(8,128)(2,1)S(1)}, bf16[1024,512]{1,0:T(8,128)(2,1)}, u32[]{:S(2)}) copy-start(bf16[1024,512]{1,0:T(8,128)(2,1)} %nodes_ref.3) | copy-start | bytes 3145732
  2.8 1.4 %copy-start.4 = (bf16[512,1536]{1,0:T(8,128)(2,1)S(1)}, bf16[512,1536]{1,0:T(8,128)(2,1)}, u32[]{:S(2)}) copy-start(bf16[512,1536]{1,0:T(8,128)(2,1)} %w_ref.1) | copy-start | bytes 4718596
  4.2 1.0 %copy-start.6 = (s32[1024,128]{1,0:T(8,128)S(1)}, s32[1024,128]{1,0:T(8,128)}, u32[]{:S(2)}) copy-start(s32[1024,128]{1,0:T(8,128)} %adj_ref.1) | copy-start | bytes 1572868
  5.2 0.7 copy-start.7
  5.9 68.5 %copy-start.1 = (bf16[1024,512]{1,0:T(8,128)(2,1)S(1)}, bf16[1024,512]{1,0:T(8,128)(2,1)}, u32[]{:S(2)}) copy-start(bf16[1024,512]{1,0:T(8,128)(2,1)} %nodes_ref.3) | copy-start | bytes 3145732
  5.9 68.5 %copy-start.2 = (bf16[512,2048]{1,0:T(8,128)(2,1)S(1)}, bf16[512,2048]{1,0:T(8,128)(2,1)}, u32[]{:S(2)}) copy-start(bf16[512,2048]{1,0:T(8,128)(2,1)} %w_up_ref.1) | copy-start | bytes 6291460
  5.9 68.5 %copy-start.5 = (bf16[512,512]{1,0:T(8,128)(2,1)S(1)}, bf16[512,512]{1,0:T(8,128)(2,1)}, u32[]{:S(2)}) copy-start(bf16[512,512]{1,0:T(8,128)(2,1)} %w_out_ref.1) | copy-start | bytes 1572868
  5.9 68.5 %copy-start.8 = (f32[512]{0:T(512)S(1)}, f32[512]{0:T(512)}, u32[]{:S(2)}) copy-start(f32[512]{0:T(512)} %param.14) | copy-start | bytes 6148
  74.4 1.6 %copy-start.3 = (bf16[2048,512]{1,0:T(8,128)(2,1)S(1)}, bf16[2048,512]{1,0:T(8,128)(2,1)}, u32[]{:S(2)}) copy-start(bf16[2048,512]{1,0:T(8,128)(2,1)} %w_down_ref.1) | copy-start | bytes 6291460

commit v2 on v1

--- a/solution.py
+++ b/solution.py
@@ -41,11 +41,18 @@
 
 def attention_kernel(
     row_size, col_size,
-    ids_ref, live_ref, nodes_ref, gain_ref, w_ref, adj_ref,
+    ids_ref, live_ref, nodes_hbm, gain_ref, w_hbm, adj_hbm,
     mixed_ref,
+    nodes_ref, w_ref, adj_ref,
     send_buf, recv_buf, dead_ref, wq_t, wv_t, q_t, keys, vals_t, keys_r, vals_r, bias_t, top, acc,
-    send_sem, recv_sem,
+    send_sem, recv_sem, load_sem,
 ):
+    loads = [
+        pltpu.make_async_copy(hbm, ref, load_sem.at[i])
+        for i, (hbm, ref) in enumerate(((nodes_hbm, nodes_ref), (w_hbm, w_ref), (adj_hbm, adj_ref)))
+    ]
+    for load in loads:
+        load.start()
     rows, width = nodes_ref.shape
     local_blocks = rows // BLK
     slots = ids_ref.shape[1]
@@ -57,19 +64,31 @@
     count = len(offsets)
     group = 2 if count % 2 == 0 else 1
 
+    def partner(me_there, d, size, sign):
+        if size & (size - 1) == 0:
+            flipped = me_there
+            bit = 1
+            while bit < size:
+                if d & bit:
+                    flipped = flipped + bit - 2 * bit * lax.rem(me_there // bit, 2)
+                bit *= 2
+            return flipped
+        return lax.rem(me_there + size + sign * d, size)
+
     def target(axis, d):
         if axis == "row":
-            return lax.rem(my_row + d, row_size), my_col
-        return my_row, lax.rem(my_col + d, col_size)
+            return partner(my_row, d, row_size, 1), my_col
+        return my_row, partner(my_col, d, col_size, 1)
 
     def source(axis, d):
         if axis == "row":
-            return lax.rem(my_row + row_size - d, row_size), my_col
-        return my_row, lax.rem(my_col + col_size - d, col_size)
+            return partner(my_row, d, row_size, -1), my_col
+        return my_row, partner(my_col, d, col_size, -1)
 
     barrier = pltpu.get_barrier_semaphore()
     for axis, d in offsets:
         pl.semaphore_signal(barrier, inc=1, device_id=target(axis, d), device_id_type=MESH)
+    loads[0].wait()
     for p, (axis, d) in enumerate(offsets):
         t_row, t_col = target(axis, d)
         peer = t_row * col_size + t_col
@@ -105,10 +124,13 @@
             dead = jnp.where(hit, jnp.float32(0), dead)
         dead_ref[p] = dead
 
+    loads[1].wait()
+    loads[2].wait()
     gain = gain_ref[...]
     wq_t[...] = w_ref[:, :width].T
     wv_t[...] = w_ref[:, 2 * width :].T
     chunk = 2 * BLK
+    wide = 2 * BLK
     score_scale = LOG2E / math.sqrt(HEAD_DIM)
     zeros = jnp.zeros((HEAD_DIM, chunk), jnp.bfloat16)
     vals_t[:, HEAD_DIM:, :] = jnp.ones((HEADS, AUG - HEAD_DIM, rows), jnp.bfloat16)
@@ -140,13 +162,14 @@
         bias_t[:, b * BLK : (b + 1) * BLK] = jnp.where(allowed, 0.0, NEG_FILL).T
 
     def attend_local(h, carry):
-        for b in range(local_blocks):
-            span = slice(b * BLK, (b + 1) * BLK)
-            score = dot(keys[h // 2, span, :], q_t[h, :, span]) + bias_t[:, span]
-            high = jnp.max(score, axis=0, keepdims=True)
-            prob = jnp.exp2(score - high).astype(jnp.bfloat16)
+        spans = [slice(b * BLK, (b + 1) * BLK) for b in range(local_blocks)]
+        scores = [dot(keys[h // 2, span, :], q_t[h, :, span]) + bias_t[:, span] for span in spans]
+        highs = [jnp.max(score, axis=0, keepdims=True) for score in scores]
+        probs = [jnp.exp2(score - high).astype(jnp.bfloat16) for score, high in zip(scores, highs)]
+        news = [dot(vals_t[h, :, span], prob) for span, prob in zip(spans, probs)]
+        for span, high, new in zip(spans, highs, news):
             top[h, :, span] = high
-            acc[h, :, span] = dot(vals_t[h, :, span], prob)
+            acc[h, :, span] = new
         return carry
 
     lax.fori_loop(0, HEADS, attend_local, 0)
@@ -166,23 +189,32 @@
         deads = [dead_ref[g * group + k] for k in range(group)]
 
         def one_head(h, inner):
-            for c in range(rows // chunk):
-                span = slice(c * chunk, (c + 1) * chunk)
-                score = dot(keys_r[h // 2], q_t[h, :, span])
-                parts = [score[k * BLK : (k + 1) * BLK] for k in range(group)]
-                old = top[h, :, span]
+            spans = [slice(c * wide, (c + 1) * wide) for c in range(rows // wide)]
+            olds = [top[h, :, span] for span in spans]
+            sums = [acc[h, :, span] for span in spans]
+            value = vals_r[h]
+            scores = [dot(keys_r[h // 2], q_t[h, :, span]) for span in spans]
+            highs = []
+            for score, old in zip(scores, olds):
                 high = old
-                for part, dead in zip(parts, deads):
+                for k, dead in enumerate(deads):
+                    part = score[k * BLK : (k + 1) * BLK]
                     high = jnp.maximum(high, jnp.max(part, axis=0, keepdims=True) + dead)
-                prob = jnp.concatenate(
+                highs.append(high)
+            probs = [
+                jnp.concatenate(
                     [
-                        jnp.exp2(part - (high - dead)).astype(jnp.bfloat16)
-                        for part, dead in zip(parts, deads)
+                        jnp.exp2(score[k * BLK : (k + 1) * BLK] - (high - dead)).astype(jnp.bfloat16)
+                        for k, dead in enumerate(deads)
                     ],
                     axis=0,
                 )
+                for score, high in zip(scores, highs)
+            ]
+            news = [dot(value, prob) for prob in probs]
+            for span, old, high, before, new in zip(spans, olds, highs, sums, news):
                 top[h, :, span] = high
-                acc[h, :, span] = acc[h, :, span] * jnp.exp2(old - high) + dot(vals_r[h], prob)
+                acc[h, :, span] = before * jnp.exp2(old - high) + new
             return inner
 
         return lax.fori_loop(0, HEADS, one_head, carry)
@@ -217,13 +249,17 @@
     group = 2 if count % 2 == 0 else 1
     vmem = pl.BlockSpec(memory_space=pltpu.VMEM)
     smem = pl.BlockSpec(memory_space=pltpu.SMEM)
+    hbm = pl.BlockSpec(memory_space=pl.ANY)
     bf16, f32 = jnp.bfloat16, jnp.float32
     mixed = pl.pallas_call(
         functools.partial(attention_kernel, row_size, col_size),
         out_shape=jax.ShapeDtypeStruct((HEADS, HEAD_DIM, rows), bf16),
-        in_specs=[smem, smem, vmem, vmem, vmem, vmem],
+        in_specs=[smem, smem, hbm, vmem, hbm, hbm],
         out_specs=vmem,
         scratch_shapes=[
+            pltpu.VMEM((rows, width), bf16),
+            pltpu.VMEM(w_qkv.shape, bf16),
+            pltpu.VMEM(adjacency.shape, adjacency.dtype),
             pltpu.VMEM((count, BLK, width), bf16),
             pltpu.VMEM((count, BLK, width), bf16),
             pltpu.SMEM((count,), f32),
@@ -239,9 +275,10 @@
             pltpu.VMEM((HEADS, AUG, rows), f32),
             pltpu.SemaphoreType.DMA((count,)),
             pltpu.SemaphoreType.DMA((count,)),
+            pltpu.SemaphoreType.DMA((3,)),
         ],
         compiler_params=pltpu.CompilerParams(
-            collective_id=0, has_side_effects=True, vmem_limit_bytes=40 << 20
+            collective_id=0, has_side_effects=True, vmem_limit_bytes=60 << 20
         ),
         name="attention",
     )(remote_ids, remote_live, nodes, ln1_gain.reshape(1, width), w_qkv, adjacency)

time: 85.2 us -> 56.7 us (0.67)
  Pallas kernels: 77.3 us -> 50.8 us
  local copies, waits for them, and re-layouts: 7.5 us -> 5.58 us
    pallas_call x1, Pallas kernels: 68.4 us -> 41.9 us  [shards(): pl.pallas_call(functools.partial(attention_kernel, row_size, col_size), o...]
    unnamed x20 -> x14, local copies, waits for them, and re-layouts: 7.5 us -> 5.58 us
where the time goes in v2:
time: 56.7 us; the launch traced here: 56.4 us
  Pallas kernels  50.8 us (90%)
  local copies, waits for them, and re-layouts  5.58 us (10%)
    pallas_call x1, Pallas kernels, shards(): pl.pallas_call(functools.partial(attention_kernel, row_size, col_size), o...  41.9 us
    pallas_call x1, Pallas kernels, shards(): pl.pallas_call(feed_kernel, grid=(rows // chunk,), out_shape=jax.ShapeDty...  8.9 us
    unnamed x14, local copies, waits for them, and re-layouts  5.58 us

profile of v2, /device:TPU:0, one launch (start us, length us, event | category | flops | bytes accessed | tf_op | source)
XLA Modules:
  0.0 56.4 jit_solution(1989592611648553398)
XLA Ops:
  0.0 1.4 %copy.11.ids_ref = s32[32,10]{1,0:T(8,128)} copy(s32[32,10]{0,1:T(8,128)} %param.18) | data formatting | bytes 2560 | tf_op args[8]
  1.4 1.4 %copy.12.live_ref = s32[32,10]{1,0:T(8,128)} copy(s32[32,10]{0,1:T(8,128)} %param.19) | data formatting | bytes 2560 | tf_op args[9]
  2.8 0.0 copy-start
  2.8 0.0 copy-start.2
  2.8 0.0 copy-start.4
  2.8 0.0 copy-start.5
  2.8 41.9 %attention.1.mixed_ref = bf16[8,64,1024]{2,1,0:T(8,128)(2,1)} custom-call(s32[32,10]{1,0:T(8,128)} %copy.11.ids_ref, s32[32,10]{1,0:T(8,128)} %copy.12.live_ref, bf16[1024,512]{1,0:T(8,128)(2,1)} %nodes_ref.1, f32[1,512]{1,0:T(1,128)} %bitcast.3, bf16[512,1536]{1,0:T(8,128)(2,1)} %w_hbm.1, s32[1024,128]{1,0:T(8,128)} %adj_hbm.1), custom_call_target="tpu_custom_call" | custom-call | tf_op jit(solution)/shard_map/attention/pallas_call | solution.py:254
  44.6 0.0 copy-done
  44.6 0.0 copy-done.2
  44.7 0.0 copy-done.4
  44.7 0.0 copy-done.5
  44.7 0.0 copy-start.1
  44.7 1.2 %copy-done.1 = bf16[8,64,1024]{2,1,0:T(8,128)(2,1)S(1)} copy-done((bf16[8,64,1024]{2,1,0:T(8,128)(2,1)S(1)}, bf16[8,64,1024]{2,1,0:T(8,128)(2,1)}, u32[]{:S(2)}) %copy-start.1) | copy-done | bytes 1048600
  45.9 0.0 copy-start.3
  45.9 1.6 %copy-done.3 = bf16[2048,512]{1,0:T(8,128)(2,1)S(1)} copy-done((bf16[2048,512]{1,0:T(8,128)(2,1)S(1)}, bf16[2048,512]{1,0:T(8,128)(2,1)}, u32[]{:S(2)}) %copy-start.3) | copy-done | bytes 2097176
  47.5 8.9 %feed.1 = bf16[1024,512]{1,0:T(8,128)(2,1)} custom-call(bf16[8,64,1024]{2,1,0:T(8,128)(2,1)S(1)} %copy-done.1, bf16[1024,512]{1,0:T(8,128)(2,1)S(1)} %copy-done, bf16[512,512]{1,0:T(8,128)(2,1)S(1)} %copy-done.4, f32[1,512]{1,0:T(1,128)S(1)} %bitcast.2, bf16[512,2048]{1,0:T(8,128)(2,1)S(1)} %copy-done.2, bf16[2048,512]{1,0:T(8,128)(2,1)S(1)} %copy-done.3), custom_call_target="tpu_custom_call" | custom-call | tf_op jit(solution)/shard_map/feed/pallas_call | solution.py:288
Async XLA Ops:
  2.8 41.9 %copy-start = (bf16[1024,512]{1,0:T(8,128)(2,1)S(1)}, bf16[1024,512]{1,0:T(8,128)(2,1)}, u32[]{:S(2)}) copy-start(bf16[1024,512]{1,0:T(8,128)(2,1)} %nodes_ref.1) | copy-start | bytes 3145732
  2.8 41.9 %copy-start.2 = (bf16[512,2048]{1,0:T(8,128)(2,1)S(1)}, bf16[512,2048]{1,0:T(8,128)(2,1)}, u32[]{:S(2)}) copy-start(bf16[512,2048]{1,0:T(8,128)(2,1)} %w_up_ref.1) | copy-start | bytes 6291460
  2.8 41.9 %copy-start.4 = (bf16[512,512]{1,0:T(8,128)(2,1)S(1)}, bf16[512,512]{1,0:T(8,128)(2,1)}, u32[]{:S(2)}) copy-start(bf16[512,512]{1,0:T(8,128)(2,1)} %w_out_ref.1) | copy-start | bytes 1572868
  2.8 41.9 %copy-start.5 = (f32[512]{0:T(512)S(1)}, f32[512]{0:T(512)}, u32[]{:S(2)}) copy-start(f32[512]{0:T(512)} %param.14) | copy-start | bytes 6148
  44.7 1.2 %copy-start.1 = (bf16[8,64,1024]{2,1,0:T(8,128)(2,1)S(1)}, bf16[8,64,1024]{2,1,0:T(8,128)(2,1)}, u32[]{:S(2)}) copy-start(bf16[8,64,1024]{2,1,0:T(8,128)(2,1)} %attention.1.mixed_ref) | copy-start | bytes 3145732
  45.9 1.6 %copy-start.3 = (bf16[2048,512]{1,0:T(8,128)(2,1)S(1)}, bf16[2048,512]{1,0:T(8,128)(2,1)}, u32[]{:S(2)}) copy-start(bf16[2048,512]{1,0:T(8,128)(2,1)} %w_down_ref.1) | copy-start | bytes 6291460
